TPU v7x, 256 devices: a whole 4x4x8 slice. The times are simulated.
256 devices in a mesh: bank: 8 (over y, x_lo), zero: 32 (over z, x_hi, core).
Axes of the slice: x: 4 (x_hi: 2, x_lo: 2; x = x_hi * 2 + x_lo), y: 4, z: 8, core: 2. Of those that a mesh axis runs over, the one named last changes fastest.
Arguments:
- master_gate: float32 [64, 2048, 1024], P('bank', 'zero'), may hold values from -0.25 to 0.25
- master_up: float32 [64, 2048, 1024], P('bank', 'zero'), may hold values from -0.25 to 0.25
- master_down: float32 [64, 1024, 2048], P('bank', None, 'zero'), may hold values from -0.375 to 0.375
- router_weight: float32 [2048, 64], P('zero', 'bank'), may hold values from -0.125 to 0.125
- router_gain: float32 [2048], P('zero'), may hold values from 0.25 to 1.75
Outputs:
- final_gate: bfloat16 [64, 2048, 1024], P('bank', None, 'zero')
- final_up: bfloat16 [64, 2048, 1024], P('bank', None, 'zero')
- final_down: bfloat16 [64, 1024, 2048], P('bank', 'zero')
- scale_gate: float32 [64, 1024], P('bank', 'zero')
- scale_up: float32 [64, 1024], P('bank', 'zero')
- scale_down: float32 [64, 1024], P('bank', 'zero')
- serve_router: bfloat16 [2048, 64], replicated
All inputs are finite; a program needn't handle non-finite values.
Results may differ from a plain program's by a relative error of at most 0.0085.
Values may be sent and summed in bfloat16 or wider, within the bound.
A program may use at most 64 MiB of HBM per device.

v0:
```python
import jax
import jax.numpy as jnp
from jax import lax
from jax.sharding import PartitionSpec as P


def from_everyone(value, axis):
    copies = jnp.broadcast_to(value, (lax.axis_size(axis), *value.shape))
    return lax.all_to_all(copies, axis, split_axis=0, concat_axis=0, tiled=True)


def over_copies(value, axis):
    everything = from_everyone(value, axis)
    return jnp.sum(everything.astype(jnp.float32), axis=0)


def sent_together(arrays, axis, split_dim, concat_dim, along):
    both = jnp.concatenate(arrays, axis=along)
    whole, at, gathered = (
        lax.all_to_all(both, axis, split_axis=split_dim, concat_axis=concat_dim, tiled=True),
        0,
        [],
    )
    for a in arrays:
        gathered.append(lax.slice_in_dim(whole, at, at + a.shape[along], axis=along))
        at += a.shape[along]
    return tuple(gathered)


def laid_out(tiles, dim):
    lengths = list(tiles.shape[1:])
    lengths[dim] *= tiles.shape[0]
    return jnp.moveaxis(tiles, 0, dim).reshape(lengths)


def gathered_copies(value, axis, dim):
    tiles = from_everyone(value, axis)
    return laid_out(tiles, dim)


def local(master_gate, master_up, master_down, router_weight, router_gain):
    total_gate, total_up, total_down = (
        over_copies(jnp.sum(master_gate * master_gate, axis=1).astype(jnp.bfloat16), "zero").astype(
            jnp.float32
        ),
        over_copies(jnp.sum(master_up * master_up, axis=1).astype(jnp.bfloat16), "zero").astype(
            jnp.float32
        ),
        over_copies(jnp.sum(master_down * master_down, axis=2).astype(jnp.bfloat16), "zero").astype(
            jnp.float32
        ),
    )
    scale_gate = jnp.sqrt(total_gate)
    scale_up = jnp.sqrt(total_up)
    scale_down = jnp.sqrt(total_down)
    narrow_gate, narrow_up, narrow_down = (
        (master_gate / jnp.expand_dims(scale_gate, 1)).astype(jnp.bfloat16),
        (master_up / jnp.expand_dims(scale_up, 1)).astype(jnp.bfloat16),
        (master_down / jnp.expand_dims(scale_down, 2)).astype(jnp.bfloat16),
    )
    final_gate, final_up = sent_together((narrow_gate, narrow_up), "zero", 2, 1, 0)
    final_down = lax.all_to_all(narrow_down, "zero", split_axis=1, concat_axis=2, tiled=True)
    scale_gate = lax.dynamic_slice_in_dim(
        scale_gate, lax.axis_index("zero") * final_gate.shape[2], final_gate.shape[2], axis=1
    )
    scale_up = lax.dynamic_slice_in_dim(
        scale_up, lax.axis_index("zero") * final_up.shape[2], final_up.shape[2], axis=1
    )
    scale_down = lax.dynamic_slice_in_dim(
        scale_down, lax.axis_index("zero") * final_down.shape[1], final_down.shape[1], axis=1
    )
    part_router = (router_weight * router_gain[:, None]).astype(jnp.bfloat16)
    row_router = gathered_copies(part_router, "zero", 0)
    serve_router = gathered_copies(row_router, "bank", 1)
    return (final_gate, final_up, final_down, scale_gate, scale_up, scale_down, serve_router)


def solution(mesh):
    in_specs = (
        P("bank", "zero", None),
        P("bank", "zero", None),
        P("bank", None, "zero"),
        P("zero", "bank"),
        P("zero"),
    )
    out_specs = (
        P("bank", None, "zero"),
        P("bank", None, "zero"),
        P("bank", "zero", None),
        P("bank", "zero"),
        P("bank", "zero"),
        P("bank", "zero"),
        P(),
    )
    return jax.shard_map(local, mesh=mesh, in_specs=in_specs, out_specs=out_specs, check_vma=False)
```

profile of v0, /device:TPU:1, one launch (start us, length us, event | category | flops | bytes accessed | tf_op | source)
XLA Modules:
  0.0 214.5 jit_solution(11568245509490080332)
XLA Ops:
  0.6 0.7 multiply_convert_fusion
  1.5 22.0 %all_to_all.58 = bf16[32,2,256]{2,1,0:T(2,128)(2,1)S(1)} all-to-all(bf16[32,2,256]{2,1,0:T(2,128)(2,1)S(1)} %reshape.38), channel_id=1, replica_groups=mesh['bank'=8,'zero'=32] {'zero'}, dimensions={0} | all-to-all | bytes 65536 | tf_op jit(solution)/shard_map/all_to_all | solution.py:9
  23.6 0.1 reshape.32
  23.7 0.7 broadcast_in_dim.23
  24.4 4.4 %all-to-all-start.6 = ((bf16[8,2048,8]{1,2,0:T(8,128)(2,1)}), bf16[8,2048,8]{1,2,0:T(8,128)(2,1)S(1)}, u32[]{:S(2)}, u32[]{:S(2)}) async-start(bf16[8,2048,8]{1,2,0:T(8,128)(2,1)} %broadcast_in_dim.23), calls=%async_computation.6 | async-start | bytes 524288 | tf_op jit(solution)/shard_map/all_to_all | solution.py:9
  28.8 1.9 multiply_reduce_fusion
  30.7 4.8 %all-to-all-done.6 = bf16[8,2048,8]{1,2,0:T(8,128)(2,1)S(1)} async-done(((bf16[8,2048,8]{1,2,0:T(8,128)(2,1)}), bf16[8,2048,8]{1,2,0:T(8,128)(2,1)S(1)}, u32[]{:S(2)}, u32[]{:S(2)}) %all-to-all-start.6) | async-done | bytes 262176 | tf_op jit(solution)/shard_map/all_to_all | solution.py:9
  35.5 0.9 broadcast_in_dim.21
  36.4 5.1 %all-to-all-start.3 = ((bf16[32,8,1024]{2,1,0:T(8,128)(2,1)}), bf16[32,8,1024]{2,1,0:T(8,128)(2,1)S(1)}, u32[]{:S(2)}, u32[]{:S(2)}) async-start(bf16[32,8,1024]{2,1,0:T(8,128)(2,1)} %broadcast_in_dim.21), calls=%async_computation.3 | async-start | bytes 1048576 | tf_op jit(solution)/shard_map/all_to_all | solution.py:9
  41.4 0.3 multiply_reduce_fusion.1
  41.7 17.0 %all-to-all-done.3 = bf16[32,8,1024]{2,1,0:T(8,128)(2,1)S(1)} async-done(((bf16[32,8,1024]{2,1,0:T(8,128)(2,1)}), bf16[32,8,1024]{2,1,0:T(8,128)(2,1)S(1)}, u32[]{:S(2)}, u32[]{:S(2)}) %all-to-all-start.3) | async-done | bytes 524320 | tf_op jit(solution)/shard_map/all_to_all | solution.py:9
  58.7 0.9 broadcast_in_dim.20
  59.6 5.5 %all-to-all-start.1 = ((bf16[32,8,1024]{2,1,0:T(8,128)(2,1)}), bf16[32,8,1024]{2,1,0:T(8,128)(2,1)S(1)}, u32[]{:S(2)}, u32[]{:S(2)}) async-start(bf16[32,8,1024]{2,1,0:T(8,128)(2,1)} %broadcast_in_dim.20), calls=%async_computation.1 | async-start | bytes 1048576 | tf_op jit(solution)/shard_map/all_to_all | solution.py:9
  65.1 2.0 multiply_reduce_fusion.2
  67.1 14.8 %all-to-all-done.1 = bf16[32,8,1024]{2,1,0:T(8,128)(2,1)S(1)} async-done(((bf16[32,8,1024]{2,1,0:T(8,128)(2,1)}), bf16[32,8,1024]{2,1,0:T(8,128)(2,1)S(1)}, u32[]{:S(2)}, u32[]{:S(2)}) %all-to-all-start.1) | async-done | bytes 524320 | tf_op jit(solution)/shard_map/all_to_all | solution.py:9
  81.9 0.9 broadcast_in_dim.19
  82.8 5.9 %all-to-all-start = ((bf16[32,8,1024]{2,1,0:T(8,128)(2,1)}), bf16[32,8,1024]{2,1,0:T(8,128)(2,1)}, u32[]{:S(2)}, u32[]{:S(2)}) async-start(bf16[32,8,1024]{2,1,0:T(8,128)(2,1)} %broadcast_in_dim.19), calls=%async_computation | async-start | bytes 1048576 | tf_op jit(solution)/shard_map/all_to_all | solution.py:9
  88.7 2.7 %copy.54 = f32[8,1024,64]{2,0,1:T(8,128)} copy(f32[8,1024,64]{1,2,0:T(8,128)S(1)} %copy-done) | data formatting | bytes 4194304 | tf_op args[2]
  91.6 0.2 copy.53
  91.8 3.9 %fusion.2 = bf16[1024,8,64]{2,1,0:T(8,128)(2,1)} fusion(f32[8,1024,64]{2,0,1:T(8,128)} %copy.54, f32[8,1024]{0,1:T(8,128)S(1)} %copy.53), kind=kLoop, calls=%fused_computation.16 | loop fusion | flops 1048576 | bytes 3178496
  95.6 4.8 %reshape.36 = bf16[32,2,8192]{2,1,0:T(2,128)(2,1)} reshape(bf16[1024,8,64]{2,1,0:T(8,128)(2,1)} %fusion.2) | data formatting | bytes 2097152
  100.4 5.2 %all-to-all-done = bf16[32,8,1024]{2,1,0:T(8,128)(2,1)} async-done(((bf16[32,8,1024]{2,1,0:T(8,128)(2,1)}), bf16[32,8,1024]{2,1,0:T(8,128)(2,1)}, u32[]{:S(2)}, u32[]{:S(2)}) %all-to-all-start) | async-done | bytes 524320 | tf_op jit(solution)/shard_map/all_to_all | solution.py:9
  105.6 5.8 %all-to-all-start.4 = ((bf16[32,2,8192]{2,1,0:T(2,128)(2,1)}), bf16[32,2,8192]{2,1,0:T(2,128)(2,1)S(1)}, u32[]{:S(2)}, u32[]{:S(2)}) async-start(bf16[32,2,8192]{2,1,0:T(2,128)(2,1)} %reshape.36), calls=%async_computation.4 | async-start | bytes 2097152 | tf_op jit(solution)/shard_map/all_to_all | solution.py:62
  111.4 2.8 %copy.47 = f32[8,64,1024]{1,0,2:T(8,128)} copy(f32[8,64,1024]{2,1,0:T(8,128)S(1)} %copy-done.1) | data formatting | bytes 4194304 | tf_op args[0]
  114.2 3.9 %copy.49 = f32[8,64,1024]{1,0,2:T(8,128)} copy(f32[8,64,1024]{2,1,0:T(8,128)} %param.6) | data formatting | bytes 4194304 | tf_op args[1]
  118.2 1.1 convert_reduce_fusion.2
  119.3 0.2 copy.46
  119.5 0.2 copy.48
  119.8 6.2 %divide_convert_fusion.1 = (bf16[8,64,1024]{1,0,2:T(8,128)(2,1)S(1)}, bf16[8,64,1024]{1,0,2:T(8,128)(2,1)S(1)}) fusion(f32[8,64,1024]{1,0,2:T(8,128)} %copy.49, f32[8,1024]{0,1:T(8,128)S(1)} %copy.48, f32[8,64,1024]{1,0,2:T(8,128)} %copy.47, f32[8,1024]{0,1:T(8,128)S(1)} %copy.46), kind=kLoop, calls=%fused_computation.2 | loop fusion | flops 2097152 | bytes 6356992 | tf_op jit(solution)/shard_map/convert_element_type | solution.py:58
  126.0 2.9 %fusion.1 = bf16[1024,16,64]{2,1,0:T(8,128)(2,1)} fusion(bf16[8,64,1024]{1,0,2:T(8,128)(2,1)S(1)} %get-tuple-element.9, bf16[8,64,1024]{1,0,2:T(8,128)(2,1)S(1)} %get-tuple-element.10), kind=kLoop, calls=%fused_computation.15 | loop fusion | flops 4194304 | bytes 4194304
  128.8 7.9 %reshape.34 = bf16[32,2,16384]{2,1,0:T(2,128)(2,1)} reshape(bf16[1024,16,64]{2,1,0:T(8,128)(2,1)} %fusion.1) | data formatting | bytes 4194304
  136.7 2.8 %all-to-all-done.4 = bf16[32,2,8192]{2,1,0:T(2,128)(2,1)S(1)} async-done(((bf16[32,2,8192]{2,1,0:T(2,128)(2,1)}), bf16[32,2,8192]{2,1,0:T(2,128)(2,1)S(1)}, u32[]{:S(2)}, u32[]{:S(2)}) %all-to-all-start.4) | async-done | bytes 1048608 | tf_op jit(solution)/shard_map/all_to_all | solution.py:62
  139.5 7.0 %all-to-all-start.2 = ((bf16[32,2,16384]{2,1,0:T(2,128)(2,1)}), bf16[32,2,16384]{2,1,0:T(2,128)(2,1)S(1)}, u32[]{:S(2)}, u32[]{:S(2)}) async-start(bf16[32,2,16384]{2,1,0:T(2,128)(2,1)} %reshape.34), calls=%async_computation.2 | async-start | bytes 4194304 | tf_op jit(solution)/shard_map/all_to_all | solution.py:20
  146.5 0.7 constant_dynamic-slice_fusion
  147.2 0.7 constant_dynamic-slice_fusion.1
  147.8 0.7 constant_dynamic-slice_fusion.2
  148.5 2.4 %reshape.37 = bf16[1024,8,64]{2,1,0:T(8,128)(2,1)} reshape(bf16[32,2,8192]{2,1,0:T(2,128)(2,1)S(1)} %all-to-all-done.4) | data formatting | bytes 2097152
  150.8 4.2 %copy.56 = bf16[8,32,32,64]{3,2,1,0:T(8,128)(2,1)} copy(bf16[8,32,32,64]{3,0,1,2:T(8,128)(2,1)} %bitcast.32) | data formatting | bytes 2097152 | tf_op jit(solution)/shard_map/all_to_all | solution.py:62
  155.1 4.2 %all_to_all.48 = bf16[8,32,2048]{2,1,0:T(8,128)(2,1)} reshape(bf16[8,32,32,64]{3,2,1,0:T(8,128)(2,1)} %copy.56) | data formatting | bytes 2097152 | tf_op jit(solution)/shard_map/all_to_all | solution.py:62
  159.3 37.1 %all-to-all-done.2 = bf16[32,2,16384]{2,1,0:T(2,128)(2,1)S(1)} async-done(((bf16[32,2,16384]{2,1,0:T(2,128)(2,1)}), bf16[32,2,16384]{2,1,0:T(2,128)(2,1)S(1)}, u32[]{:S(2)}, u32[]{:S(2)}) %all-to-all-start.2) | async-done | bytes 2097184 | tf_op jit(solution)/shard_map/all_to_all | solution.py:20
  196.4 4.0 %reshape.35 = bf16[1024,16,64]{2,1,0:T(8,128)(2,1)} reshape(bf16[32,2,16384]{2,1,0:T(2,128)(2,1)S(1)} %all-to-all-done.2) | data formatting | bytes 4194304
  200.4 3.3 %copy.50 = bf16[16,64,1024]{1,2,0:T(8,128)(2,1)S(1)} copy(bf16[16,64,1024]{1,0,2:T(8,128)(2,1)} %bitcast.31) | data formatting | bytes 4194304 | tf_op jit(solution)/shard_map/all_to_all | solution.py:20
  203.6 2.1 fusion
  205.7 0.8 copy.51
  206.5 2.4 %slice.13 = bf16[8,2048,32]{1,2,0:T(8,128)(2,1)} reshape(bf16[8,32,64,32]{2,1,3,0:T(8,128)(2,1)S(1)} %copy.51) | data formatting | bytes 2097152 | tf_op jit(solution)/shard_map/slice | solution.py:25
  209.0 2.4 %copy.52 = bf16[8,32,64,32]{2,1,3,0:T(8,128)(2,1)S(1)} copy(bf16[8,32,64,32]{2,3,1,0:T(8,128)(2,1)} %get-tuple-element.7) | data formatting | bytes 2097152 | tf_op jit(solution)/shard_map/slice | solution.py:25
  211.4 2.4 %slice.15 = bf16[8,2048,32]{1,2,0:T(8,128)(2,1)} reshape(bf16[8,32,64,32]{2,1,3,0:T(8,128)(2,1)S(1)} %copy.52) | data formatting | bytes 2097152 | tf_op jit(solution)/shard_map/slice | solution.py:25
  213.8 0.7 copy.60
  (19 shorter events, 0.5 us)
Async XLA Ops:
  24.4 17.0 %copy-start.2 = (f32[8,64,1024]{2,1,0:T(8,128)S(1)}, f32[8,64,1024]{2,1,0:T(8,128)}, u32[]{:S(2)}) copy-start(f32[8,64,1024]{2,1,0:T(8,128)} %param.6) | copy-start | bytes 6291460
  24.4 11.0 %all-to-all-start.6 = ((bf16[8,2048,8]{1,2,0:T(8,128)(2,1)}), bf16[8,2048,8]{1,2,0:T(8,128)(2,1)S(1)}, u32[]{:S(2)}, u32[]{:S(2)}) async-start(bf16[8,2048,8]{1,2,0:T(8,128)(2,1)} %broadcast_in_dim.23), calls=%async_computation.6 | async-start | bytes 524288 | tf_op jit(solution)/shard_map/all_to_all | solution.py:9
  36.4 22.4 %all-to-all-start.3 = ((bf16[32,8,1024]{2,1,0:T(8,128)(2,1)}), bf16[32,8,1024]{2,1,0:T(8,128)(2,1)S(1)}, u32[]{:S(2)}, u32[]{:S(2)}) async-start(bf16[32,8,1024]{2,1,0:T(8,128)(2,1)} %broadcast_in_dim.21), calls=%async_computation.3 | async-start | bytes 1048576 | tf_op jit(solution)/shard_map/all_to_all | solution.py:9
  59.6 22.3 %all-to-all-start.1 = ((bf16[32,8,1024]{2,1,0:T(8,128)(2,1)}), bf16[32,8,1024]{2,1,0:T(8,128)(2,1)S(1)}, u32[]{:S(2)}, u32[]{:S(2)}) async-start(bf16[32,8,1024]{2,1,0:T(8,128)(2,1)} %broadcast_in_dim.20), calls=%async_computation.1 | async-start | bytes 1048576 | tf_op jit(solution)/shard_map/all_to_all | solution.py:9
  65.1 23.6 %copy-start = (f32[8,1024,64]{1,2,0:T(8,128)S(1)}, f32[8,1024,64]{1,2,0:T(8,128)}, u32[]{:S(2)}) copy-start(f32[8,1024,64]{1,2,0:T(8,128)} %param.7) | copy-start | bytes 6291460
  81.9 9.5 %copy-start.3 = (bf16[32,8,1024]{2,1,0:T(8,128)(2,1)}, bf16[32,8,1024]{2,1,0:T(8,128)(2,1)S(1)}, u32[]{:S(2)}) copy-start(bf16[32,8,1024]{2,1,0:T(8,128)(2,1)S(1)} %all-to-all-done.1) | copy-start | bytes 1572868
  82.8 22.8 %all-to-all-start = ((bf16[32,8,1024]{2,1,0:T(8,128)(2,1)}), bf16[32,8,1024]{2,1,0:T(8,128)(2,1)}, u32[]{:S(2)}, u32[]{:S(2)}) async-start(bf16[32,8,1024]{2,1,0:T(8,128)(2,1)} %broadcast_in_dim.19), calls=%async_computation | async-start | bytes 1048576 | tf_op jit(solution)/shard_map/all_to_all | solution.py:9
  95.6 15.8 %copy-start.1 = (f32[8,64,1024]{2,1,0:T(8,128)S(1)}, f32[8,64,1024]{2,1,0:T(8,128)}, u32[]{:S(2)}) copy-start(f32[8,64,1024]{2,1,0:T(8,128)} %param.5) | copy-start | bytes 6291460
  105.6 33.9 %all-to-all-start.4 = ((bf16[32,2,8192]{2,1,0:T(2,128)(2,1)}), bf16[32,2,8192]{2,1,0:T(2,128)(2,1)S(1)}, u32[]{:S(2)}, u32[]{:S(2)}) async-start(bf16[32,2,8192]{2,1,0:T(2,128)(2,1)} %reshape.36), calls=%async_computation.4 | async-start | bytes 2097152 | tf_op jit(solution)/shard_map/all_to_all | solution.py:62
  114.2 3.9 %copy-start.4 = (bf16[32,8,1024]{2,1,0:T(8,128)(2,1)S(1)}, bf16[32,8,1024]{2,1,0:T(8,128)(2,1)}, u32[]{:S(2)}) copy-start(bf16[32,8,1024]{2,1,0:T(8,128)(2,1)} %copy-done.3) | copy-start | bytes 1572868
  139.5 56.9 %all-to-all-start.2 = ((bf16[32,2,16384]{2,1,0:T(2,128)(2,1)}), bf16[32,2,16384]{2,1,0:T(2,128)(2,1)S(1)}, u32[]{:S(2)}, u32[]{:S(2)}) async-start(bf16[32,2,16384]{2,1,0:T(2,128)(2,1)} %reshape.34), calls=%async_computation.2 | async-start | bytes 4194304 | tf_op jit(solution)/shard_map/all_to_all | solution.py:20
where the time goes:
time: 216 us; the launch traced here: 214 us
  waiting for transfers between devices  81.7 us (38%)
  local copies, waits for them, and re-layouts  57.3 us (27%)
  starting transfers between devices  33.5 us (16%)
  blocking collectives  22 us (10%)
  other arithmetic  19.1 us (9%)
    all_to_all x4, waiting for transfers between devices, from_everyone(): return lax.all_to_all(copies, axis, split_axis=0, concat_axis=0, tiled=True)  41.8 us
    all_to_all x1, waiting for transfers between devices, sent_together(): lax.all_to_all(both, axis, split_axis=split_dim, concat_axis=concat_dim,...  37.1 us
    unnamed x21, local copies, waits for them, and re-layouts  29.3 us
    all_to_all x1, blocking collectives, from_everyone(): return lax.all_to_all(copies, axis, split_axis=0, concat_axis=0, tiled=True)  22 us
    all_to_all x4, starting transfers between devices, from_everyone(): return lax.all_to_all(copies, axis, split_axis=0, concat_axis=0, tiled=True)  20.8 us
    slice x5, local copies, waits for them, and re-layouts, sent_together(): lax.slice_in_dim(whole, at, at + a.shape[along], axis=along)  10.1 us
    all_to_all x2, local copies, waits for them, and re-layouts, local(): lax.all_to_all(narrow_down, 'zero', split_axis=1, concat_axis=2, tiled=True)  8.47 us
    all_to_all x1, starting transfers between devices, sent_together(): lax.all_to_all(both, axis, split_axis=split_dim, concat_axis=concat_dim,...  6.96 us
  transfers between devices with their start and end apart: 6, of which 6 were waited for; matrix products, arithmetic and copies ran while one was open for 23% of the time, Pallas kernels for 0%

commit v1 on v0

v1 whole, which is shorter than its diff:
```python
import functools

import jax
import jax.numpy as jnp
from jax import lax
from jax.experimental import pallas as pl
from jax.experimental.pallas import tpu as pltpu
from jax.sharding import PartitionSpec as P

MESH = pl.DeviceIdType.MESH
ZERO, BANK = 32, 8
CHIPS = ZERO // 2
HEADS = 8
PAIRS = 12
ROWS, COLS, PIECE, LANES = 64, 1024, 32, 128


def zero_peer(me, step):
    z, x, core = me // 4, (me // 2) % 2, me % 2
    turn = step // 4
    away = (turn + 1) // 2
    dz = jnp.where(turn % 2 == 1, 4 - away, 4 + away)
    dx = 1 - (step // 2) % 2
    dc = 1 - step % 2
    return ((z + dz) % 8) * 4 + ((x + dx) % 2) * 2 + (core + dc) % 2


def exchange(
    gate, up, down, router_hbm, gain_hbm,
    final, scales, served,
    held, router, gain, send, recv, mine, other, rows,
    load_sem, send_sem, recv_sem, own_sem, pair_sem, row_sem, bank_sem, small_sem,
):
    me, bank = lax.axis_index("zero"), lax.axis_index("bank")
    core, chip = me % 2, me // 2
    sources = (gate, up, down)

    def load(p):
        source = sources[p // 4]
        return pltpu.make_async_copy(source.at[pl.ds((p % 4) * LANES, LANES)], held.at[p], load_sem.at[p])

    load(0).start()
    small = (
        pltpu.make_async_copy(router_hbm, router, small_sem.at[0]),
        pltpu.make_async_copy(gain_hbm, gain, small_sem.at[1]),
    )
    for copy in small:
        copy.start()
    for p in range(1, PAIRS):
        load(p).start()

    barrier = pltpu.get_barrier_semaphore()

    def greet(step, _):
        pl.semaphore_signal(barrier, inc=1, device_id={"zero": zero_peer(me, step)}, device_id_type=MESH)
        return 0

    lax.fori_loop(0, ZERO - 1, greet, 0)
    for step in range(1, BANK):
        pl.semaphore_signal(barrier, inc=1, device_id={"bank": (bank + step) % BANK}, device_id_type=MESH)

    half = lax.broadcasted_iota(jnp.int32, (PIECE, LANES), 1) < ROWS
    for copy in small:
        copy.wait()
    part = (router[...] * gain[...]).astype(jnp.bfloat16)
    mine[...] = jnp.concatenate([part, part], axis=1)

    def prepare(p):
        def block(q, _):
            at = pl.multiple_of(q * LANES, LANES)
            turned = held[p, :, pl.ds(at, LANES)].T.astype(jnp.bfloat16)
            send[p, pl.ds(q * 4, 4)] = turned.reshape(4, PIECE, LANES)
            return 0

        lax.fori_loop(0, COLS // LANES, block, 0)

    def start(p):
        def one(step, _):
            peer = zero_peer(me, step)
            pltpu.make_async_remote_copy(
                src_ref=send.at[p, peer], dst_ref=recv.at[p, me], send_sem=send_sem.at[p],
                recv_sem=recv_sem.at[p], device_id={"zero": peer}, device_id_type=MESH,
            ).start()
            return 0

        lax.fori_loop(0, ZERO - 1, one, 0)
        pltpu.make_async_copy(send.at[p, me], recv.at[p, me], own_sem.at[p]).start()

    load(0).wait()
    prepare(0)
    pl.semaphore_wait(barrier, ZERO - 1 + BANK - 1)

    to_pair = pltpu.make_async_remote_copy(
        src_ref=mine, dst_ref=other, send_sem=pair_sem.at[0], recv_sem=pair_sem.at[1],
        device_id={"zero": chip * 2 + 1 - core}, device_id_type=MESH,
    )
    to_pair.start()
    start(0)

    to_pair.wait()
    lower = lax.broadcasted_iota(jnp.int32, (HEADS, LANES), 1) < ROWS
    keep_mine = jnp.where(lower, 0, 1) == core
    at_chip = pl.ds(pl.multiple_of(chip * LANES, LANES), LANES)
    rows[:, at_chip] = jnp.where(
        keep_mine, mine[...].astype(jnp.float32), other[...].astype(jnp.float32)
    ).astype(jnp.bfloat16)

    def row_copy(step):
        return pltpu.make_async_remote_copy(
            src_ref=rows.at[:, at_chip], dst_ref=rows.at[:, at_chip], send_sem=row_sem.at[0],
            recv_sem=row_sem.at[1], device_id={"zero": ((chip + step) % CHIPS) * 2 + core}, device_id_type=MESH,
        )

    for step in range(1, CHIPS):
        row_copy(step).start()

    for p in range(1, PAIRS):
        load(p).wait()
        prepare(p)
        start(p)

    others = rows.at[:, pl.ds(0, (CHIPS - 1) * LANES)]
    pltpu.make_async_copy(others, others, row_sem.at[1]).wait()

    def bank_copy(step):
        return pltpu.make_async_remote_copy(
            src_ref=rows, dst_ref=served.at[bank], send_sem=bank_sem.at[0],
            recv_sem=bank_sem.at[1], device_id={"bank": (bank + step) % BANK}, device_id_type=MESH,
        )

    for step in range(1, BANK):
        bank_copy(step).start()
    served[bank] = rows[...]

    lane = lax.broadcasted_iota(jnp.int32, (PIECE, LANES), 1)

    def finish(p, kept):
        pltpu.make_async_copy(send.at[p, me], recv.at[p, me], own_sem.at[p]).wait()
        arrived = pltpu.make_async_copy(recv.at[p, pl.ds(0, ZERO - 1)], recv.at[p, pl.ds(0, ZERO - 1)], recv_sem.at[p])
        arrived.wait()

        def square(k, total):
            a = recv[p, 2 * k].astype(jnp.float32)
            b = recv[p, 2 * k + 1].astype(jnp.float32)
            return total + (a * a + b * b)

        total = lax.fori_loop(0, CHIPS, square, jnp.zeros((PIECE, LANES), jnp.float32), unroll=4)
        first = jnp.sqrt(jnp.sum(jnp.where(half, total, 0.0), axis=1, keepdims=True))
        second = jnp.sqrt(jnp.sum(jnp.where(half, 0.0, total), axis=1, keepdims=True))
        factor = 1.0 / jnp.where(half, first, second)

        def spread(k, _):
            a = recv[p, 2 * k].astype(jnp.float32) * factor
            b = recv[p, 2 * k + 1].astype(jnp.float32) * factor
            at = pl.ds(pl.multiple_of(k * LANES, LANES), LANES)
            final[2 * p, :, at] = jnp.where(half, a, pltpu.roll(b, ROWS, 1)).astype(jnp.bfloat16)
            final[2 * p + 1, :, at] = jnp.where(half, pltpu.roll(a, ROWS, 1), b).astype(jnp.bfloat16)
            return 0

        lax.fori_loop(0, CHIPS, spread, 0, unroll=4)
        return jnp.where(lane == 2 * p, first, jnp.where(lane == 2 * p + 1, second, kept))

    kept = lax.fori_loop(0, PAIRS, finish, jnp.zeros((PIECE, LANES), jnp.float32))
    scales[...] = kept.T[: 2 * PAIRS, :]

    pltpu.make_async_copy(others, others, row_sem.at[0]).wait()
    blocks = served.at[pl.ds(0, BANK - 1)]
    pltpu.make_async_copy(blocks, blocks, bank_sem.at[0]).wait()
    pltpu.make_async_copy(blocks, blocks, bank_sem.at[1]).wait()
    for p in range(PAIRS):
        pltpu.make_async_copy(send.at[p, pl.ds(0, ZERO - 1)], send.at[p, pl.ds(0, ZERO - 1)], send_sem.at[p]).wait()


def write_out(final, scales, served, gate, up, down, scale_gate, scale_up, scale_down, router, sems):
    copies = []
    for i, (to_final, to_scale) in enumerate(((gate, scale_gate), (up, scale_up), (down, scale_down))):
        at = pl.ds(i * HEADS, HEADS)
        copies.append(pltpu.make_async_copy(final.at[at], to_final, sems.at[2 * i]))
        copies.append(pltpu.make_async_copy(scales.at[at], to_scale, sems.at[2 * i + 1]))
    copies.append(pltpu.make_async_copy(served, router, sems.at[6]))
    for copy in copies:
        copy.start()
    for copy in copies:
        copy.wait()


def local(master_gate, master_up, master_down, router_weight, router_gain):
    gate = master_gate.reshape(HEADS * ROWS, COLS)
    up = master_up.reshape(HEADS * ROWS, COLS)
    down = jnp.transpose(master_down, (0, 2, 1)).reshape(HEADS * ROWS, COLS)
    router = router_weight.T
    gain = router_gain.reshape(1, ROWS)
    anywhere = pl.BlockSpec(memory_space=pl.ANY)
    vmem = pl.BlockSpec(memory_space=pltpu.VMEM)
    wide = CHIPS * LANES
    held = (
        jax.ShapeDtypeStruct((2 * PAIRS, PIECE, wide), jnp.bfloat16),
        jax.ShapeDtypeStruct((2 * PAIRS, PIECE), jnp.float32),
        jax.ShapeDtypeStruct((BANK, HEADS, wide), jnp.bfloat16),
    )
    final, scales, served = pl.pallas_call(
        exchange,
        out_shape=held,
        in_specs=[pl.BlockSpec(memory_space=pltpu.HBM)] * 5,
        out_specs=(vmem,) * 3,
        scratch_shapes=[
            pltpu.VMEM((PAIRS, LANES, COLS), jnp.float32),
            pltpu.VMEM((HEADS, ROWS), jnp.float32),
            pltpu.VMEM((1, ROWS), jnp.float32),
            pltpu.VMEM((PAIRS, ZERO, PIECE, LANES), jnp.bfloat16),
            pltpu.VMEM((PAIRS, ZERO, PIECE, LANES), jnp.bfloat16),
            pltpu.VMEM((HEADS, LANES), jnp.bfloat16),
            pltpu.VMEM((HEADS, LANES), jnp.bfloat16),
            pltpu.VMEM((HEADS, wide), jnp.bfloat16),
            pltpu.SemaphoreType.DMA((PAIRS,)),
            pltpu.SemaphoreType.DMA((PAIRS,)),
            pltpu.SemaphoreType.DMA((PAIRS,)),
            pltpu.SemaphoreType.DMA((PAIRS,)),
            pltpu.SemaphoreType.DMA((2,)),
            pltpu.SemaphoreType.DMA((2,)),
            pltpu.SemaphoreType.DMA((2,)),
            pltpu.SemaphoreType.DMA((2,)),
        ],
        compiler_params=pltpu.CompilerParams(
            collective_id=0, has_side_effects=True, vmem_limit_bytes=24 * 2**20
        ),
        name="exchange",
    )(*(pltpu.with_memory_space_constraint(a, pltpu.HBM) for a in (gate, up, down, router, gain)))
    piece = jax.ShapeDtypeStruct((HEADS, PIECE, wide), jnp.bfloat16)
    scale = jax.ShapeDtypeStruct((HEADS, PIECE), jnp.float32)
    outs = pl.pallas_call(
        write_out,
        out_shape=(piece, piece, piece, scale, scale, scale, held[2]),
        in_specs=[vmem] * 3,
        out_specs=(anywhere,) * 7,
        scratch_shapes=[pltpu.SemaphoreType.DMA((7,))],
        compiler_params=pltpu.CompilerParams(vmem_limit_bytes=8 * 2**20),
        name="write_out",
    )(final, scales, served)
    final_gate, final_up, final_down, scale_gate, scale_up, scale_down, router_out = outs
    serve_router = router_out.reshape(BANK * HEADS, wide).T
    return (
        jnp.transpose(final_gate, (0, 2, 1)), jnp.transpose(final_up, (0, 2, 1)), final_down,
        scale_gate, scale_up, scale_down, serve_router,
    )


def solution(mesh):
    in_specs = (
        P("bank", "zero", None),
        P("bank", "zero", None),
        P("bank", None, "zero"),
        P("zero", "bank"),
        P("zero"),
    )
    out_specs = (
        P("bank", None, "zero"),
        P("bank", None, "zero"),
        P("bank", "zero", None),
        P("bank", "zero"),
        P("bank", "zero"),
        P("bank", "zero"),
        P(),
    )
    return jax.shard_map(local, mesh=mesh, in_specs=in_specs, out_specs=out_specs, check_vma=False)
```

time: 216 us -> 86.5 us (0.40)
  Pallas kernels: 0 us -> 85.8 us
  waiting for transfers between devices: 81.7 us -> 0 us
  local copies, waits for them, and re-layouts: 57.3 us -> 0 us
  starting transfers between devices: 33.5 us -> 0 us
  blocking collectives: 22 us -> 0 us
  other arithmetic: 19.1 us -> 0 us
    pallas_call x0 -> x2, Pallas kernels: none -> 85.8 us  [the longest x1 83.9 us: local(): pl.pallas_call(exchange, out_shape=held, in_specs=[pl.BlockSpec(memory_sp...]
    all_to_all x6 -> x0, waiting for transfers between devices: 81.7 us -> none  [the longest x4 41.8 us: from_everyone(): return lax.all_to_all(copies, axis, split_axis=0, concat_axis=0, tiled=True)]
    all_to_all x6 -> x0, starting transfers between devices: 33.5 us -> none  [the longest x4 20.8 us: from_everyone(): return lax.all_to_all(copies, axis, split_axis=0, concat_axis=0, tiled=True)]
    unnamed x21 -> x0, local copies, waits for them, and re-layouts: 29.3 us -> none
    all_to_all x1 -> x0, blocking collectives: 22 us -> none  [from_everyone(): return lax.all_to_all(copies, axis, split_axis=0, concat_axis=0, tiled=True)]
    all_to_all x4 -> x0, local copies, waits for them, and re-layouts: 11.8 us -> none  [the longest x2 8.47 us: local(): lax.all_to_all(narrow_down, 'zero', split_axis=1, concat_axis=2, tiled=True)]
    slice x5 -> x0, local copies, waits for them, and re-layouts: 10.1 us -> none  [sent_together(): lax.slice_in_dim(whole, at, at + a.shape[along], axis=along)]
    convert_element_type x2 -> x0, other arithmetic: 6.88 us -> none  [the longest x1 6.19 us: local(): (master_up / jnp.expand_dims(scale_up, 1)).astype(jnp.bfloat16)]
  transfers between devices with their start and end apart: 6 -> 0, of which waited for: 6 -> 0; matrix products, arithmetic and copies ran while one was open for 23% -> 0% of each run, Pallas kernels for 0% -> 0%
where the time goes in v1:
time: 86.5 us; the launch traced here: 86.4 us
  Pallas kernels  85.8 us (99%)
    pallas_call x1, Pallas kernels, local(): pl.pallas_call(exchange, out_shape=held, in_specs=[pl.BlockSpec(memory_sp...  83.9 us
    pallas_call x1, Pallas kernels, local(): pl.pallas_call(write_out, out_shape=(piece, piece, piece, scale, scale, s...  1.81 us

profile of v1, /device:TPU:1, one launch (start us, length us, event | category | flops | bytes accessed | tf_op | source)
XLA Modules:
  0.0 86.4 jit_solution(5548732131340466730)
XLA Ops:
  0.6 83.9 %exchange.1 = (bf16[24,32,2048]{2,1,0:T(8,128)(2,1)S(1)}, f32[24,32]{1,0:T(8,128)S(1)}, bf16[8,8,2048]{2,1,0:T(8,128)(2,1)S(1)}) custom-call(f32[512,1024]{1,0:T(8,128)} %bitcast.12, f32[512,1024]{1,0:T(8,128)} %bitcast.13, f32[512,1024]{1,0:T(8,128)} %bitcast.14, f32[8,64]{1,0:T(8,128)} %bitcast.15, f32[1,64]{1,0:T(1,128)} %bitcast.16), custom_call_target="tpu_custom_call" | custom-call | tf_op jit(solution)/shard_map/exchange/pallas_call | solution.py:201
  84.6 1.8 %write_out.1 = (bf16[8,32,2048]{2,1,0:T(8,128)(2,1)}, bf16[8,32,2048]{2,1,0:T(8,128)(2,1)}, bf16[8,32,2048]{2,1,0:T(8,128)(2,1)}, f32[8,32]{1,0:T(8,128)}, f32[8...) custom-call(bf16[24,32,2048]{2,1,0:T(8,128)(2,1)S(1)} %get-tuple-element.17.final, ...), custom_call_target="tpu_custom_call" | custom-call | tf_op jit(solution)/shard_map/write_out/pallas_call | solution.py:231

commit v2 on v1

v2 whole, which is shorter than its diff:
```python
import functools

import jax
import jax.numpy as jnp
from jax import lax
from jax.experimental import pallas as pl
from jax.experimental.pallas import tpu as pltpu
from jax.sharding import PartitionSpec as P

MESH = pl.DeviceIdType.MESH
ZERO, BANK = 32, 8
CHIPS = ZERO // 2
HEADS = 8
PAIRS = 12
ROWS, COLS, PIECE, LANES = 64, 1024, 32, 128


TURNS = (4, 3, 5, 2, 6, 1, 7, 0)


def interleave(recv, factor, half, final, first, second):
    def spread(k, _):
        a = recv[2 * k].astype(jnp.float32) * factor
        b = recv[2 * k + 1].astype(jnp.float32) * factor
        at = pl.ds(pl.multiple_of(k * LANES, LANES), LANES)
        final[first, :, at] = jnp.where(half, a, pltpu.roll(b, ROWS, 1)).astype(jnp.bfloat16)
        final[second, :, at] = jnp.where(half, pltpu.roll(a, ROWS, 1), b).astype(jnp.bfloat16)
        return 0

    lax.fori_loop(0, CHIPS, spread, 0, unroll=4)


def finish(recv, p, final, first, second, kept):
    lane = lax.broadcasted_iota(jnp.int32, (PIECE, LANES), 1)
    half = lane < ROWS

    def square(k, total):
        a = recv[2 * k].astype(jnp.float32)
        b = recv[2 * k + 1].astype(jnp.float32)
        return total + (a * a + b * b)

    total = lax.fori_loop(0, CHIPS, square, jnp.zeros((PIECE, LANES), jnp.float32), unroll=4)
    low = jnp.sqrt(jnp.sum(jnp.where(half, total, 0.0), axis=1, keepdims=True))
    high = jnp.sqrt(jnp.sum(jnp.where(half, 0.0, total), axis=1, keepdims=True))
    interleave(recv, 1.0 / jnp.where(half, low, high), half, final, first, second)
    return jnp.where(lane == 2 * p, low, jnp.where(lane == 2 * p + 1, high, kept))


def exchange(
    gate, up, down, router_hbm, gain_hbm,
    final, last, scales, served,
    held, router, gain, send, recv, mine, other, rows,
    load_sem, send_sem, recv_sem, own_sem, pair_sem, row_sem, bank_sem, small_sem,
):
    me, bank = lax.axis_index("zero"), lax.axis_index("bank")
    z, low = lax.div(me, 4), lax.rem(me, 4)
    x, core, chip = lax.div(low, 2), lax.rem(me, 2), lax.div(me, 2)
    planes = [lax.rem(z + dz, 8) for dz in TURNS]
    places = [(1 - x) * 2 + 1 - core, (1 - x) * 2 + core, x * 2 + 1 - core, low]
    sources = (gate, up, down)

    def load(p):
        source = sources[p // 4]
        return pltpu.make_async_copy(source.at[pl.ds((p % 4) * LANES, LANES)], held.at[p], load_sem.at[p])

    load(0).start()
    barrier = pltpu.get_barrier_semaphore()
    for turn, plane in enumerate(planes):
        for place in places[: 3 if TURNS[turn] == 0 else 4]:
            pl.semaphore_signal(barrier, inc=1, device_id={"zero": plane * 4 + place}, device_id_type=MESH)
    for step in range(1, BANK):
        pl.semaphore_signal(barrier, inc=1, device_id={"bank": lax.rem(bank + step, BANK)}, device_id_type=MESH)

    small = (
        pltpu.make_async_copy(router_hbm, router, small_sem.at[0]),
        pltpu.make_async_copy(gain_hbm, gain, small_sem.at[1]),
    )
    for copy in small:
        copy.start()
    for p in range(1, PAIRS):
        load(p).start()

    def landing(p):
        return last if isinstance(p, int) and p == PAIRS - 1 else recv.at[p]

    def prepare(p, turn):
        plane = planes[turn]
        at = pl.multiple_of(plane * LANES, LANES)
        turned = held[p, :, pl.ds(at, LANES)].T.astype(jnp.bfloat16)
        send[p, pl.ds(plane * 4, 4)] = turned.reshape(4, PIECE, LANES)

    def start(p, turn):
        for place in places:
            peer = planes[turn] * 4 + place
            if TURNS[turn] == 0 and place is low:
                pltpu.make_async_copy(send.at[p, me], landing(p).at[me], own_sem.at[p]).start()
            else:
                pltpu.make_async_remote_copy(
                    src_ref=send.at[p, peer], dst_ref=landing(p).at[me], send_sem=send_sem.at[p],
                    recv_sem=recv_sem.at[p], device_id={"zero": peer}, device_id_type=MESH,
                ).start()

    load(0).wait()
    prepare(0, 0)
    prepare(0, 1)
    pl.semaphore_wait(barrier, ZERO - 1 + BANK - 1)
    for turn in range(8):
        if turn + 2 < 8:
            prepare(0, turn + 2)
        start(0, turn)

    for copy in small:
        copy.wait()
    part = (router[...] * gain[...]).astype(jnp.bfloat16)
    mine[...] = jnp.concatenate([part, part], axis=1)
    to_pair = pltpu.make_async_remote_copy(
        src_ref=mine, dst_ref=other, send_sem=pair_sem.at[0], recv_sem=pair_sem.at[1],
        device_id={"zero": chip * 2 + 1 - core}, device_id_type=MESH,
    )

    def prepare_and_start(p):
        load_p = pltpu.make_async_copy(gate.at[pl.ds(0, LANES)], held.at[p], load_sem.at[p])
        load_p.wait()
        prepare(p, 0)
        for turn in range(8):
            if turn + 1 < 8:
                prepare(p, turn + 1)
            start(p, turn)

    prepare_and_start(1)
    to_pair.start()
    prepare_and_start(2)
    to_pair.wait()
    lower = lax.broadcasted_iota(jnp.int32, (HEADS, LANES), 1) < ROWS
    keep_mine = jnp.where(lower, 0, 1) == core
    at_chip = pl.ds(pl.multiple_of(chip * LANES, LANES), LANES)
    rows[:, at_chip] = jnp.where(
        keep_mine, mine[...].astype(jnp.float32), other[...].astype(jnp.float32)
    ).astype(jnp.bfloat16)

    def row_copy(step):
        return pltpu.make_async_remote_copy(
            src_ref=rows.at[:, at_chip], dst_ref=rows.at[:, at_chip], send_sem=row_sem.at[0],
            recv_sem=row_sem.at[1], device_id={"zero": lax.rem(chip + step, CHIPS) * 2 + core}, device_id_type=MESH,
        )

    prepare_and_start(3)
    for step in range(1, CHIPS):
        row_copy(step).start()

    def next_pair(p, _):
        prepare_and_start(p)
        return 0

    lax.fori_loop(4, PAIRS - 1, next_pair, 0)
    prepare_and_start(PAIRS - 1)

    others = rows.at[:, pl.ds(0, (CHIPS - 1) * LANES)]
    pltpu.make_async_copy(others, others, row_sem.at[1]).wait()

    def bank_copy(step):
        return pltpu.make_async_remote_copy(
            src_ref=rows, dst_ref=served.at[bank], send_sem=bank_sem.at[0],
            recv_sem=bank_sem.at[1], device_id={"bank": lax.rem(bank + step, BANK)}, device_id_type=MESH,
        )

    for step in range(1, BANK):
        bank_copy(step).start()
    served[bank] = rows[...]

    def arrive(p):
        pieces = landing(p)
        pltpu.make_async_copy(send.at[p, me], pieces.at[me], own_sem.at[p]).wait()
        arrived = pieces.at[pl.ds(0, ZERO - 1)]
        pltpu.make_async_copy(arrived, arrived, recv_sem.at[p]).wait()
        sent = send.at[p, pl.ds(0, ZERO - 1)]
        pltpu.make_async_copy(sent, sent, send_sem.at[p]).wait()

    def take(p, kept):
        arrive(p)
        return finish(recv.at[p], p, final, 2 * p, 2 * p + 1, kept)

    scales[...] = lax.fori_loop(0, PAIRS - 1, take, jnp.zeros((PIECE, LANES), jnp.float32))
    pltpu.make_async_copy(others, others, row_sem.at[0]).wait()
    blocks = served.at[pl.ds(0, BANK - 1)]
    pltpu.make_async_copy(blocks, blocks, bank_sem.at[0]).wait()
    pltpu.make_async_copy(blocks, blocks, bank_sem.at[1]).wait()
    arrive(PAIRS - 1)


def write_out(
    final, last, scales, served,
    gate, up, down, scale_gate, scale_up, scale_down, router,
    tail, turned, sems,
):
    copies = []

    def put(source, target):
        copy = pltpu.make_async_copy(source, target, sems.at[len(copies)])
        copy.start()
        copies.append(copy)

    put(final.at[pl.ds(0, 8)], gate)
    put(final.at[pl.ds(8, 8)], up)
    put(final.at[pl.ds(16, 6)], down.at[pl.ds(0, 6)])
    put(served, router)
    kept = finish(last, PAIRS - 1, tail, 0, 1, scales[...])
    put(tail, down.at[pl.ds(6, 2)])
    turned[...] = kept.T[: 2 * PAIRS, :]
    for i, target in enumerate((scale_gate, scale_up, scale_down)):
        put(turned.at[pl.ds(i * HEADS, HEADS)], target)
    for copy in copies:
        copy.wait()


def local(master_gate, master_up, master_down, router_weight, router_gain):
    gate = master_gate.reshape(HEADS * ROWS, COLS)
    up = master_up.reshape(HEADS * ROWS, COLS)
    down = jnp.transpose(master_down, (0, 2, 1)).reshape(HEADS * ROWS, COLS)
    router = router_weight.T
    gain = router_gain.reshape(1, ROWS)
    anywhere = pl.BlockSpec(memory_space=pl.ANY)
    vmem = pl.BlockSpec(memory_space=pltpu.VMEM)
    wide = CHIPS * LANES
    held = (
        jax.ShapeDtypeStruct((2 * PAIRS - 2, PIECE, wide), jnp.bfloat16),
        jax.ShapeDtypeStruct((ZERO, PIECE, LANES), jnp.bfloat16),
        jax.ShapeDtypeStruct((PIECE, LANES), jnp.float32),
        jax.ShapeDtypeStruct((BANK, HEADS, wide), jnp.bfloat16),
    )
    final, last, scales, served = pl.pallas_call(
        exchange,
        out_shape=held,
        in_specs=[pl.BlockSpec(memory_space=pltpu.HBM)] * 5,
        out_specs=(vmem,) * 4,
        scratch_shapes=[
            pltpu.VMEM((PAIRS, LANES, COLS), jnp.float32),
            pltpu.VMEM((HEADS, ROWS), jnp.float32),
            pltpu.VMEM((1, ROWS), jnp.float32),
            pltpu.VMEM((PAIRS, ZERO, PIECE, LANES), jnp.bfloat16),
            pltpu.VMEM((PAIRS - 1, ZERO, PIECE, LANES), jnp.bfloat16),
            pltpu.VMEM((HEADS, LANES), jnp.bfloat16),
            pltpu.VMEM((HEADS, LANES), jnp.bfloat16),
            pltpu.VMEM((HEADS, wide), jnp.bfloat16),
            pltpu.SemaphoreType.DMA((PAIRS,)),
            pltpu.SemaphoreType.DMA((PAIRS,)),
            pltpu.SemaphoreType.DMA((PAIRS,)),
            pltpu.SemaphoreType.DMA((PAIRS,)),
            pltpu.SemaphoreType.DMA((2,)),
            pltpu.SemaphoreType.DMA((2,)),
            pltpu.SemaphoreType.DMA((2,)),
            pltpu.SemaphoreType.DMA((2,)),
        ],
        compiler_params=pltpu.CompilerParams(
            collective_id=0, has_side_effects=True, vmem_limit_bytes=24 * 2**20
        ),
        name="exchange",
    )(*(pltpu.with_memory_space_constraint(a, pltpu.HBM) for a in (gate, up, down, router, gain)))
    piece = jax.ShapeDtypeStruct((HEADS, PIECE, wide), jnp.bfloat16)
    scale = jax.ShapeDtypeStruct((HEADS, PIECE), jnp.float32)
    outs = pl.pallas_call(
        write_out,
        out_shape=(piece, piece, piece, scale, scale, scale, held[3]),
        in_specs=[vmem] * 4,
        out_specs=(anywhere,) * 7,
        scratch_shapes=[
            pltpu.VMEM((2, PIECE, wide), jnp.bfloat16),
            pltpu.VMEM((2 * PAIRS, PIECE), jnp.float32),
            pltpu.SemaphoreType.DMA((8,)),
        ],
        compiler_params=pltpu.CompilerParams(vmem_limit_bytes=8 * 2**20),
        name="write_out",
    )(final, last, scales, served)
    final_gate, final_up, final_down, scale_gate, scale_up, scale_down, router_out = outs
    serve_router = router_out.reshape(BANK * HEADS, wide).T
    return (
        jnp.transpose(final_gate, (0, 2, 1)), jnp.transpose(final_up, (0, 2, 1)), final_down,
        scale_gate, scale_up, scale_down, serve_router,
    )


def solution(mesh):
    in_specs = (
        P("bank", "zero", None),
        P("bank", "zero", None),
        P("bank", None, "zero"),
        P("zero", "bank"),
        P("zero"),
    )
    out_specs = (
        P("bank", None, "zero"),
        P("bank", None, "zero"),
        P("bank", "zero", None),
        P("bank", "zero"),
        P("bank", "zero"),
        P("bank", "zero"),
        P(),
    )
    return jax.shard_map(local, mesh=mesh, in_specs=in_specs, out_specs=out_specs, check_vma=False)
```

time: 86.5 us -> 84.9 us (0.982)
  Pallas kernels: 85.8 us -> 84.2 us
    pallas_call x1, Pallas kernels: 83.9 us -> 82.4 us  [local(): pl.pallas_call(exchange, out_shape=held, in_specs=[pl.BlockSpec(memory_sp...]
where the time goes in v2:
time: 84.9 us; the launch traced here: 84.8 us
  Pallas kernels  84.2 us (99%)
    pallas_call x1, Pallas kernels, local(): pl.pallas_call(exchange, out_shape=held, in_specs=[pl.BlockSpec(memory_sp...  82.4 us
    pallas_call x1, Pallas kernels, local(): pl.pallas_call(write_out, out_shape=(piece, piece, piece, scale, scale, s...  1.82 us

profile of v2, /device:TPU:1, one launch (start us, length us, event | category | flops | bytes accessed | tf_op | source)
XLA Modules:
  0.0 84.8 jit_solution(8004075312046079448)
XLA Ops:
  0.6 82.4 %exchange.1 = (bf16[22,32,2048]{2,1,0:T(8,128)(2,1)S(1)}, bf16[32,32,128]{2,1,0:T(8,128)(2,1)S(1)}, f32[32,128]{1,0:T(8,128)S(1)}, bf16[8,8,2048]{2,1,0:T(8,128)(2,1)S(1)}) custom-call(f32[512,1024]{1,0:T(8,128)} %bitcast.12, f32[512,1024]{1,0:T(8,128)} %bitcast.13, f32[512,1024]{1,0:T(8,128)} %bitcast.14, f32[8,64]{1,0:T(8,128)} %bitcast.15, f32[1,64]{1,0:T(1,128)} %bitcast.16), custom_call_target="tpu_custom_call" | custom-call | tf_op jit(solution)/shard_map/exchange/pallas_call | solution.py:231
  83.0 1.8 %write_out.1 = (bf16[8,32,2048]{2,1,0:T(8,128)(2,1)}, bf16[8,32,2048]{2,1,0:T(8,128)(2,1)}, bf16[8,32,2048]{2,1,0:T(8,128)(2,1)}, f32[8,32]{1,0:T(8,128)}, f32[8...) custom-call(bf16[22,32,2048]{2,1,0:T(8,128)(2,1)S(1)} %get-tuple-element.18.final, ...), custom_call_target="tpu_custom_call" | custom-call | tf_op jit(solution)/shard_map/write_out/pallas_call | solution.py:261

commit v3 on v2

v3 whole, which is shorter than its diff:
```python
import functools

import jax
import jax.numpy as jnp
from jax import lax
from jax.experimental import pallas as pl
from jax.experimental.pallas import tpu as pltpu
from jax.sharding import PartitionSpec as P

MESH = pl.DeviceIdType.MESH
ZERO, BANK = 32, 8
CHIPS = ZERO // 2
HEADS = 8
PAIRS = 12
CHUNKS, EACH = 6, 2
ROWS, COLS, PIECE, LANES = 64, 1024, 32, 128


NEAR = (1, -1, 0)
TURNS = (4, 3, -3, 2, -2, 1, -1, 0)
EARLY = 2


def interleave(recv, i, factor, half, final, first, second):
    def spread(k, _):
        a = recv[2 * k, i].astype(jnp.float32) * factor
        b = recv[2 * k + 1, i].astype(jnp.float32) * factor
        at = pl.ds(pl.multiple_of(k * LANES, LANES), LANES)
        final[first, :, at] = jnp.where(half, a, pltpu.roll(b, ROWS, 1)).astype(jnp.bfloat16)
        final[second, :, at] = jnp.where(half, pltpu.roll(a, ROWS, 1), b).astype(jnp.bfloat16)
        return 0

    lax.fori_loop(0, CHIPS, spread, 0, unroll=16)


def finish(recv, i, p, final, first, second, kept):
    lane = lax.broadcasted_iota(jnp.int32, (PIECE, LANES), 1)
    half = lane < ROWS

    def square(k, total):
        a = recv[2 * k, i].astype(jnp.float32)
        b = recv[2 * k + 1, i].astype(jnp.float32)
        return total + (a * a + b * b)

    total = lax.fori_loop(0, CHIPS, square, jnp.zeros((PIECE, LANES), jnp.float32), unroll=16)
    low = jnp.sqrt(jnp.sum(jnp.where(half, total, 0.0), axis=1, keepdims=True))
    high = jnp.sqrt(jnp.sum(jnp.where(half, 0.0, total), axis=1, keepdims=True))
    interleave(recv, i, 1.0 / jnp.where(half, low, high), half, final, first, second)
    return jnp.where(lane == 2 * p, low, jnp.where(lane == 2 * p + 1, high, kept))


def exchange(
    gate, up, down, router_hbm, gain_hbm,
    final, last, scales, served,
    held, router, gain, send, recv, mine, other, column, beside, rows,
    load_sem, send_sem, recv_sem, pair_sem, column_sem, beside_sem, bank_sem, small_sem, news,
):
    me, bank = lax.axis_index("zero"), lax.axis_index("bank")
    z, low = lax.div(me, 4), lax.rem(me, 4)
    x, core = lax.div(low, 2), lax.rem(me, 2)
    places = [(1 - x) * 2 + 1 - core, (1 - x) * 2 + core, x * 2 + 1 - core, low]
    sources = (gate, up, down)

    down_first = jnp.where(lax.rem(z + 2, 8) < 4, 0, 1)
    way = 1 - 2 * down_first

    def plane(dz):
        return lax.rem(z + 8 + way * dz, 8)

    def load(c):
        source, size = sources[c // 2], EACH * LANES
        return pltpu.make_async_copy(source.at[pl.ds((c % 2) * size, size)], held.at[c], load_sem.at[c])

    load(0).start()
    barrier = pltpu.get_barrier_semaphore()
    greeted = 0
    for dz in NEAR:
        for place in places[:3] if dz == 0 else places[2:]:
            pl.semaphore_signal(barrier, inc=1, device_id={"zero": plane(dz) * 4 + place}, device_id_type=MESH)
            greeted += 1
    for step in range(1, BANK):
        pl.semaphore_signal(barrier, inc=1, device_id={"bank": lax.rem(bank + step, BANK)}, device_id_type=MESH)
        greeted += 1

    small = (
        pltpu.make_async_copy(router_hbm, router, small_sem.at[0]),
        pltpu.make_async_copy(gain_hbm, gain, small_sem.at[1]),
    )
    for copy in small:
        copy.start()
    for c in range(1, CHUNKS):
        load(c).start()

    def landing(c):
        return last if isinstance(c, int) and c == CHUNKS - 1 else recv.at[c]

    def prepare(c, dz):
        at = pl.multiple_of(plane(dz) * LANES, LANES)
        for i in range(EACH):
            turned = held[c, pl.ds(i * LANES, LANES), pl.ds(at, LANES)].T.astype(jnp.bfloat16)
            send[c, pl.ds(plane(dz) * 4, 4), i] = turned.reshape(4, PIECE, LANES)

    def start(c, dz, some=slice(None)):
        for place in places[some]:
            peer = plane(dz) * 4 + place
            if dz == 0 and place is low:
                pltpu.make_async_copy(send.at[c, me], landing(c).at[me], recv_sem.at[c]).start()
            else:
                pltpu.make_async_remote_copy(
                    src_ref=send.at[c, peer], dst_ref=landing(c).at[me], send_sem=send_sem.at[0],
                    recv_sem=recv_sem.at[c], device_id={"zero": peer}, device_id_type=MESH,
                ).start()

    def heard_of(dz):
        upward = down_first if dz < 0 else 1 - down_first
        return news.at[(1 - upward) * 4 + abs(dz) - 1]

    def pass_on(dz):
        side = 1 if dz > 0 else -1
        upward = down_first if side < 0 else 1 - down_first
        target = plane(-side) * 4 + low
        pl.semaphore_signal(
            news.at[(1 - upward) * 4 + abs(dz)], inc=1, device_id={"zero": target}, device_id_type=MESH
        )

    load(0).wait()
    for dz in NEAR:
        prepare(0, dz)
    to_pair = pltpu.make_async_remote_copy(
        src_ref=mine, dst_ref=other, send_sem=pair_sem.at[0], recv_sem=pair_sem.at[1],
        device_id={"zero": z * 4 + places[2]}, device_id_type=MESH,
    )

    pl.semaphore_wait(barrier, greeted)
    for side in (1, -1):
        pl.semaphore_signal(
            news.at[down_first * 4 if side < 0 else (1 - down_first) * 4],
            inc=1, device_id={"zero": plane(side) * 4 + low}, device_id_type=MESH,
        )
    for c in range(EARLY):
        if c > 0:
            load(c).wait()
            for dz in NEAR:
                prepare(c, dz)
        for dz in NEAR:
            start(c, dz, slice(None) if dz == 0 else slice(2, None))
    for copy in small:
        copy.wait()
    part = (router[...] * gain[...]).astype(jnp.bfloat16)
    mine[...] = jnp.concatenate([part, part], axis=1)
    to_pair.start()
    for dz in (1, -1, 2, -2, 3, -3, 4, -4):
        pl.semaphore_wait(heard_of(dz), 1)
        if abs(dz) < 4:
            pass_on(dz)
        for c in range(EARLY if dz != -4 else 0):
            if abs(dz) > 1:
                prepare(c, dz)
            start(c, dz, slice(None) if abs(dz) > 1 else slice(0, 2))

    to_pair.wait()
    lower = lax.broadcasted_iota(jnp.int32, (HEADS, LANES), 1) < ROWS
    keep_mine = jnp.where(lower, 0, 1) == core
    mine[...] = jnp.where(
        keep_mine, mine[...].astype(jnp.float32), other[...].astype(jnp.float32)
    ).astype(jnp.bfloat16)

    def column_copy(dz):
        return pltpu.make_async_remote_copy(
            src_ref=mine, dst_ref=column.at[dz // 2], send_sem=column_sem.at[0], recv_sem=column_sem.at[1],
            device_id={"zero": lax.rem(z + dz, 8) * 4 + low}, device_id_type=MESH,
        )

    @pl.when(core == 0)
    def _():
        column[0] = mine[...]
        for dz in (4, 2, 6):
            column_copy(dz).start()

    @pl.when(core == 1)
    def _():
        for dz in (3, 5, 1, 7):
            column_copy(dz).start()

    def column_wait(which):
        @pl.when(core == 0)
        def _():
            pltpu.make_async_copy(column.at[pl.ds(0, 3)], column.at[pl.ds(0, 3)], column_sem.at[which]).wait()

        @pl.when(core == 1)
        def _():
            pltpu.make_async_copy(column, column, column_sem.at[which]).wait()

    def beside_copy(i):
        return pltpu.make_async_remote_copy(
            src_ref=column, dst_ref=beside.at[i], send_sem=beside_sem.at[0], recv_sem=beside_sem.at[1],
            device_id={"zero": z * 4 + places[i]}, device_id_type=MESH,
        )

    def bank_copy(step):
        return pltpu.make_async_remote_copy(
            src_ref=rows, dst_ref=served.at[bank], send_sem=bank_sem.at[0],
            recv_sem=bank_sem.at[1], device_id={"bank": lax.rem(bank + step, BANK)}, device_id_type=MESH,
        )

    def prepare_and_start(c):
        size = EACH * LANES
        pltpu.make_async_copy(gate.at[pl.ds(0, size)], held.at[c], load_sem.at[c]).wait()
        prepare(c, TURNS[0])
        for turn, dz in enumerate(TURNS):
            if turn + 1 < len(TURNS):
                prepare(c, TURNS[turn + 1])
            start(c, dz)

    def arrive(c):
        pltpu.make_async_copy(landing(c), landing(c), recv_sem.at[c]).wait()

    def take(c, kept):
        arrive(c)
        for i in range(EACH):
            p = c * EACH + i
            kept = finish(recv.at[c], i, p, final, 2 * p, 2 * p + 1, kept)
        return kept

    def step(c, kept):
        prepare_and_start(c)
        return take(c - EARLY, kept)

    kept = lax.fori_loop(EARLY, 4, step, jnp.zeros((PIECE, LANES), jnp.float32))
    column_wait(1)
    for i in range(3):
        beside_copy(i).start()
    kept = step(4, kept)
    prepare_and_start(CHUNKS - 1)
    pltpu.make_async_copy(beside, beside, beside_sem.at[1]).wait()
    for i in range(4):
        side, parity = lax.div(places[i], 2), lax.rem(places[i], 2)
        for j in range(4):
            chip = lax.rem(z + 8 - 2 * j - parity, 8) * 2 + side
            at = pl.ds(pl.multiple_of(chip * LANES, LANES), LANES)
            rows[:, at] = column[j] if i == 3 else beside[i, j]
    for peer in range(1, BANK):
        bank_copy(peer).start()
    served[bank] = rows[...]

    scales[...] = lax.fori_loop(CHUNKS - 1 - EARLY, CHUNKS - 1, take, kept)
    column_wait(0)
    pltpu.make_async_copy(beside, beside, beside_sem.at[0]).wait()
    blocks = served.at[pl.ds(0, BANK - 1)]
    pltpu.make_async_copy(blocks, blocks, bank_sem.at[0]).wait()
    pltpu.make_async_copy(blocks, blocks, bank_sem.at[1]).wait()
    arrive(CHUNKS - 1)
    sent = send.at[:, pl.ds(0, ZERO - 1)]
    pltpu.make_async_copy(sent, sent, send_sem.at[0]).wait()


def write_out(
    final, last, scales, served,
    gate, up, down, scale_gate, scale_up, scale_down, router,
    tail, turned, sems,
):
    copies = []

    def put(source, target):
        copy = pltpu.make_async_copy(source, target, sems.at[len(copies)])
        copy.start()
        copies.append(copy)

    put(final.at[pl.ds(0, 8)], gate)
    put(final.at[pl.ds(8, 8)], up)
    put(final.at[pl.ds(16, 4)], down.at[pl.ds(0, 4)])
    put(served, router)
    kept = scales[...]
    for i in range(EACH):
        kept = finish(last, i, PAIRS - EACH + i, tail, 2 * i, 2 * i + 1, kept)
        put(tail.at[pl.ds(2 * i, 2)], down.at[pl.ds(4 + 2 * i, 2)])
    turned[...] = kept.T[: 2 * PAIRS, :]
    for i, target in enumerate((scale_gate, scale_up, scale_down)):
        put(turned.at[pl.ds(i * HEADS, HEADS)], target)
    for copy in copies:
        copy.wait()


def local(master_gate, master_up, master_down, router_weight, router_gain):
    gate = master_gate.reshape(HEADS * ROWS, COLS)
    up = master_up.reshape(HEADS * ROWS, COLS)
    down = jnp.transpose(master_down, (0, 2, 1)).reshape(HEADS * ROWS, COLS)
    router = router_weight.T
    gain = router_gain.reshape(1, ROWS)
    anywhere = pl.BlockSpec(memory_space=pl.ANY)
    vmem = pl.BlockSpec(memory_space=pltpu.VMEM)
    wide = CHIPS * LANES
    held = (
        jax.ShapeDtypeStruct((2 * (PAIRS - EACH), PIECE, wide), jnp.bfloat16),
        jax.ShapeDtypeStruct((ZERO, EACH, PIECE, LANES), jnp.bfloat16),
        jax.ShapeDtypeStruct((PIECE, LANES), jnp.float32),
        jax.ShapeDtypeStruct((BANK, HEADS, wide), jnp.bfloat16),
    )
    final, last, scales, served = pl.pallas_call(
        exchange,
        out_shape=held,
        in_specs=[pl.BlockSpec(memory_space=pltpu.HBM)] * 5,
        out_specs=(vmem,) * 4,
        scratch_shapes=[
            pltpu.VMEM((CHUNKS, EACH * LANES, COLS), jnp.float32),
            pltpu.VMEM((HEADS, ROWS), jnp.float32),
            pltpu.VMEM((1, ROWS), jnp.float32),
            pltpu.VMEM((CHUNKS, ZERO, EACH, PIECE, LANES), jnp.bfloat16),
            pltpu.VMEM((CHUNKS - 1, ZERO, EACH, PIECE, LANES), jnp.bfloat16),
            pltpu.VMEM((HEADS, LANES), jnp.bfloat16),
            pltpu.VMEM((HEADS, LANES), jnp.bfloat16),
            pltpu.VMEM((4, HEADS, LANES), jnp.bfloat16),
            pltpu.VMEM((3, 4, HEADS, LANES), jnp.bfloat16),
            pltpu.VMEM((HEADS, wide), jnp.bfloat16),
            pltpu.SemaphoreType.DMA((CHUNKS,)),
            pltpu.SemaphoreType.DMA((1,)),
            pltpu.SemaphoreType.DMA((CHUNKS,)),
            pltpu.SemaphoreType.DMA((2,)),
            pltpu.SemaphoreType.DMA((2,)),
            pltpu.SemaphoreType.DMA((2,)),
            pltpu.SemaphoreType.DMA((2,)),
            pltpu.SemaphoreType.DMA((2,)),
            pltpu.SemaphoreType.REGULAR((8,)),
        ],
        compiler_params=pltpu.CompilerParams(
            collective_id=0, has_side_effects=True, vmem_limit_bytes=24 * 2**20
        ),
        name="exchange",
    )(*(pltpu.with_memory_space_constraint(a, pltpu.HBM) for a in (gate, up, down, router, gain)))
    piece = jax.ShapeDtypeStruct((HEADS, PIECE, wide), jnp.bfloat16)
    scale = jax.ShapeDtypeStruct((HEADS, PIECE), jnp.float32)
    outs = pl.pallas_call(
        write_out,
        out_shape=(piece, piece, piece, scale, scale, scale, held[3]),
        in_specs=[vmem] * 4,
        out_specs=(anywhere,) * 7,
        scratch_shapes=[
            pltpu.VMEM((2 * EACH, PIECE, wide), jnp.bfloat16),
            pltpu.VMEM((2 * PAIRS, PIECE), jnp.float32),
            pltpu.SemaphoreType.DMA((9,)),
        ],
        compiler_params=pltpu.CompilerParams(vmem_limit_bytes=8 * 2**20),
        name="write_out",
    )(final, last, scales, served)
    final_gate, final_up, final_down, scale_gate, scale_up, scale_down, router_out = outs
    serve_router = router_out.reshape(BANK * HEADS, wide).T
    return (
        jnp.transpose(final_gate, (0, 2, 1)), jnp.transpose(final_up, (0, 2, 1)), final_down,
        scale_gate, scale_up, scale_down, serve_router,
    )


def solution(mesh):
    in_specs = (
        P("bank", "zero", None),
        P("bank", "zero", None),
        P("bank", None, "zero"),
        P("zero", "bank"),
        P("zero"),
    )
    out_specs = (
        P("bank", None, "zero"),
        P("bank", None, "zero"),
        P("bank", "zero", None),
        P("bank", "zero"),
        P("bank", "zero"),
        P("bank", "zero"),
        P(),
    )
    return jax.shard_map(local, mesh=mesh, in_specs=in_specs, out_specs=out_specs, check_vma=False)
```

time: 84.9 us -> 83.4 us (0.982)
  Pallas kernels: 84.2 us -> 82.6 us
    pallas_call x1, Pallas kernels: 82.4 us -> 80.8 us  [local(): pl.pallas_call(exchange, out_shape=held, in_specs=[pl.BlockSpec(memory_sp...]
where the time goes in v3:
time: 83.4 us; the launch traced here: 83.3 us
  Pallas kernels  82.6 us (99%)
    pallas_call x1, Pallas kernels, local(): pl.pallas_call(exchange, out_shape=held, in_specs=[pl.BlockSpec(memory_sp...  80.8 us
    pallas_call x1, Pallas kernels, local(): pl.pallas_call(write_out, out_shape=(piece, piece, piece, scale, scale, s...  1.83 us

profile of v3, /device:TPU:1, one launch (start us, length us, event | category | flops | bytes accessed | tf_op | source)
XLA Modules:
  0.0 83.3 jit_solution(2864752506060199480)
XLA Ops:
  0.6 80.8 %exchange.1 = (bf16[20,32,2048]{2,1,0:T(8,128)(2,1)S(1)}, bf16[32,2,32,128]{3,2,1,0:T(8,128)(2,1)S(1)}, f32[32,128]{1,0:T(8,128)S(1)}, bf16[8,8,2048]{2,1,0:T(8,128)(2,1)S(1)}) custom-call(f32[512,1024]{1,0:T(8,128)} %bitcast.12, f32[512,1024]{1,0:T(8,128)} %bitcast.13, f32[512,1024]{1,0:T(8,128)} %bitcast.14, f32[8,64]{1,0:T(8,128)} %bitcast.15, ...), custom_call_target="tpu_custom_call" | custom-call | tf_op jit(solution)/shard_map/exchange/pallas_call | solution.py:299
  81.5 1.8 %write_out.1 = (bf16[8,32,2048]{2,1,0:T(8,128)(2,1)}, bf16[8,32,2048]{2,1,0:T(8,128)(2,1)}, bf16[8,32,2048]{2,1,0:T(8,128)(2,1)}, f32[8,32]{1,0:T(8,128)}, f32[8...) custom-call(bf16[20,32,2048]{2,1,0:T(8,128)(2,1)S(1)} %get-tuple-element.18.final, ...), custom_call_target="tpu_custom_call" | custom-call | tf_op jit(solution)/shard_map/write_out/pallas_call | solution.py:332

commit v4 on v3

--- a/solution.py
+++ b/solution.py
@@ -54,6 +54,7 @@
     final, last, scales, served,
     held, router, gain, send, recv, mine, other, column, beside, rows,
     load_sem, send_sem, recv_sem, pair_sem, column_sem, beside_sem, bank_sem, small_sem, news,
+    block_sem, whole, everyone,
 ):
     me, bank = lax.axis_index("zero"), lax.axis_index("bank")
     z, low = lax.div(me, 4), lax.rem(me, 4)
@@ -71,17 +72,31 @@
         source, size = sources[c // 2], EACH * LANES
         return pltpu.make_async_copy(source.at[pl.ds((c % 2) * size, size)], held.at[c], load_sem.at[c])
 
-    load(0).start()
+    def load_block(dz):
+        at = pl.ds(pl.multiple_of(plane(dz) * LANES, LANES), LANES)
+        return pltpu.make_async_copy(
+            gate.at[pl.ds(0, EACH * LANES), at], held.at[0, :, at], block_sem.at[TURNS.index(dz)]
+        )
+
+    for dz in NEAR:
+        load_block(dz).start()
     barrier = pltpu.get_barrier_semaphore()
-    greeted = 0
-    for dz in NEAR:
-        for place in places[:3] if dz == 0 else places[2:]:
-            pl.semaphore_signal(barrier, inc=1, device_id={"zero": plane(dz) * 4 + place}, device_id_type=MESH)
-            greeted += 1
-    for step in range(1, BANK):
-        pl.semaphore_signal(barrier, inc=1, device_id={"bank": lax.rem(bank + step, BANK)}, device_id_type=MESH)
-        greeted += 1
-
+    near = [(0, places[0]), (0, places[1]), (1, low), (-1, low), (1, places[2]), (-1, places[2]), (0, places[2])]
+    for dz, place in near:
+        pl.semaphore_signal(barrier, inc=1, device_id={"zero": plane(dz) * 4 + place}, device_id_type=MESH)
+
+    def to_banks(signalled):
+        for step in range(1, BANK):
+            pl.semaphore_signal(
+                signalled, inc=1, device_id={"bank": lax.rem(bank + step, BANK)}, device_id_type=MESH
+            )
+
+    @pl.when(z == 0)
+    def _():
+        to_banks(barrier)
+
+    for dz in (2, -2, 3, -3, 4):
+        load_block(dz).start()
     small = (
         pltpu.make_async_copy(router_hbm, router, small_sem.at[0]),
         pltpu.make_async_copy(gain_hbm, gain, small_sem.at[1]),
@@ -123,15 +138,22 @@
             news.at[(1 - upward) * 4 + abs(dz)], inc=1, device_id={"zero": target}, device_id_type=MESH
         )
 
-    load(0).wait()
     for dz in NEAR:
+        load_block(dz).wait()
         prepare(0, dz)
     to_pair = pltpu.make_async_remote_copy(
         src_ref=mine, dst_ref=other, send_sem=pair_sem.at[0], recv_sem=pair_sem.at[1],
         device_id={"zero": z * 4 + places[2]}, device_id_type=MESH,
     )
 
-    pl.semaphore_wait(barrier, greeted)
+    @pl.when(z == 0)
+    def _():
+        pl.semaphore_wait(barrier, len(near) + BANK - 1)
+
+    @pl.when(z != 0)
+    def _():
+        pl.semaphore_wait(barrier, len(near))
+
     for side in (1, -1):
         pl.semaphore_signal(
             news.at[down_first * 4 if side < 0 else (1 - down_first) * 4],
@@ -153,10 +175,16 @@
         pl.semaphore_wait(heard_of(dz), 1)
         if abs(dz) < 4:
             pass_on(dz)
+        if abs(dz) > 1 and dz != -4:
+            load_block(dz).wait()
+            for c in range(EARLY):
+                prepare(c, dz)
         for c in range(EARLY if dz != -4 else 0):
-            if abs(dz) > 1:
-                prepare(c, dz)
             start(c, dz, slice(None) if abs(dz) > 1 else slice(0, 2))
+
+    @pl.when(z == 0)
+    def _():
+        to_banks(whole)
 
     to_pair.wait()
     lower = lax.broadcasted_iota(jnp.int32, (HEADS, LANES), 1) < ROWS
@@ -227,6 +255,12 @@
         return take(c - EARLY, kept)
 
     kept = lax.fori_loop(EARLY, 4, step, jnp.zeros((PIECE, LANES), jnp.float32))
+    @pl.when(z == 0)
+    def _():
+        pl.semaphore_wait(whole, BANK - 1)
+        for other_z in range(1, 8):
+            pl.semaphore_signal(everyone, inc=1, device_id={"zero": other_z * 4 + low}, device_id_type=MESH)
+
     column_wait(1)
     for i in range(3):
         beside_copy(i).start()
@@ -239,6 +273,11 @@
             chip = lax.rem(z + 8 - 2 * j - parity, 8) * 2 + side
             at = pl.ds(pl.multiple_of(chip * LANES, LANES), LANES)
             rows[:, at] = column[j] if i == 3 else beside[i, j]
+
+    @pl.when(z != 0)
+    def _():
+        pl.semaphore_wait(everyone, 1)
+
     for peer in range(1, BANK):
         bank_copy(peer).start()
     served[bank] = rows[...]
@@ -321,6 +360,9 @@
             pltpu.SemaphoreType.DMA((2,)),
             pltpu.SemaphoreType.DMA((2,)),
             pltpu.SemaphoreType.REGULAR((8,)),
+            pltpu.SemaphoreType.DMA((8,)),
+            pltpu.SemaphoreType.REGULAR,
+            pltpu.SemaphoreType.REGULAR,
         ],
         compiler_params=pltpu.CompilerParams(
             collective_id=0, has_side_effects=True, vmem_limit_bytes=24 * 2**20

time: 83.4 us -> 81.8 us (0.981)
  Pallas kernels: 82.6 us -> 81.1 us
    pallas_call x1, Pallas kernels: 80.8 us -> 79.3 us  [local(): pl.pallas_call(exchange, out_shape=held, in_specs=[pl.BlockSpec(memory_sp...]
where the time goes in v4:
time: 81.8 us; the launch traced here: 81.7 us
  Pallas kernels  81.1 us (99%)
    pallas_call x1, Pallas kernels, local(): pl.pallas_call(exchange, out_shape=held, in_specs=[pl.BlockSpec(memory_sp...  79.3 us
    pallas_call x1, Pallas kernels, local(): pl.pallas_call(write_out, out_shape=(piece, piece, piece, scale, scale, s...  1.83 us

profile of v4, /device:TPU:1, one launch (start us, length us, event | category | flops | bytes accessed | tf_op | source)
XLA Modules:
  0.0 81.7 jit_solution(7999617138354372762)
XLA Ops:
  0.6 79.3 %exchange.1 = (bf16[20,32,2048]{2,1,0:T(8,128)(2,1)S(1)}, bf16[32,2,32,128]{3,2,1,0:T(8,128)(2,1)S(1)}, f32[32,128]{1,0:T(8,128)S(1)}, bf16[8,8,2048]{2,1,0:T(8,128)(2,1)S(1)}) custom-call(f32[512,1024]{1,0:T(8,128)} %bitcast.12, f32[512,1024]{1,0:T(8,128)} %bitcast.13, f32[512,1024]{1,0:T(8,128)} %bitcast.14, f32[8,64]{1,0:T(8,128)} %bitcast.15, ...), custom_call_target="tpu_custom_call" | custom-call | tf_op jit(solution)/shard_map/exchange/pallas_call | solution.py:338
  79.9 1.8 %write_out.1 = (bf16[8,32,2048]{2,1,0:T(8,128)(2,1)}, bf16[8,32,2048]{2,1,0:T(8,128)(2,1)}, bf16[8,32,2048]{2,1,0:T(8,128)(2,1)}, f32[8,32]{1,0:T(8,128)}, f32[8...) custom-call(bf16[20,32,2048]{2,1,0:T(8,128)(2,1)S(1)} %get-tuple-element.18.final, ...), custom_call_target="tpu_custom_call" | custom-call | tf_op jit(solution)/shard_map/write_out/pallas_call | solution.py:374

commit v5 on v4

--- a/solution.py
+++ b/solution.py
@@ -18,7 +18,7 @@
 
 NEAR = (1, -1, 0)
 TURNS = (4, 3, -3, 2, -2, 1, -1, 0)
-EARLY = 2
+EARLY = 3
 
 
 def interleave(recv, i, factor, half, final, first, second):
@@ -138,7 +138,7 @@
             news.at[(1 - upward) * 4 + abs(dz)], inc=1, device_id={"zero": target}, device_id_type=MESH
         )
 
-    for dz in NEAR:
+    for dz in NEAR[:2]:
         load_block(dz).wait()
         prepare(0, dz)
     to_pair = pltpu.make_async_remote_copy(
@@ -165,6 +165,9 @@
             for dz in NEAR:
                 prepare(c, dz)
         for dz in NEAR:
+            if c == 0 and dz == 0:
+                load_block(dz).wait()
+                prepare(c, dz)
             start(c, dz, slice(None) if dz == 0 else slice(2, None))
     for copy in small:
         copy.wait()

time: 81.8 us -> 81.3 us (level)
  no operation moved by 1% of the time
where the time goes in v5:
time: 81.3 us; the launch traced here: 81.2 us
  Pallas kernels  80.6 us (99%)
    pallas_call x1, Pallas kernels, local(): pl.pallas_call(exchange, out_shape=held, in_specs=[pl.BlockSpec(memory_sp...  78.8 us
    pallas_call x1, Pallas kernels, local(): pl.pallas_call(write_out, out_shape=(piece, piece, piece, scale, scale, s...  1.83 us

profile of v5, /device:TPU:1, one launch (start us, length us, event | category | flops | bytes accessed | tf_op | source)
XLA Modules:
  0.0 81.2 jit_solution(17835860517211997650)
XLA Ops:
  0.6 78.8 %exchange.1 = (bf16[20,32,2048]{2,1,0:T(8,128)(2,1)S(1)}, bf16[32,2,32,128]{3,2,1,0:T(8,128)(2,1)S(1)}, f32[32,128]{1,0:T(8,128)S(1)}, bf16[8,8,2048]{2,1,0:T(8,128)(2,1)S(1)}) custom-call(f32[512,1024]{1,0:T(8,128)} %bitcast.12, f32[512,1024]{1,0:T(8,128)} %bitcast.13, f32[512,1024]{1,0:T(8,128)} %bitcast.14, f32[8,64]{1,0:T(8,128)} %bitcast.15, ...), custom_call_target="tpu_custom_call" | custom-call | tf_op jit(solution)/shard_map/exchange/pallas_call | solution.py:341
  79.4 1.8 %write_out.1 = (bf16[8,32,2048]{2,1,0:T(8,128)(2,1)}, bf16[8,32,2048]{2,1,0:T(8,128)(2,1)}, bf16[8,32,2048]{2,1,0:T(8,128)(2,1)}, f32[8,32]{1,0:T(8,128)}, f32[8...) custom-call(bf16[20,32,2048]{2,1,0:T(8,128)(2,1)S(1)} %get-tuple-element.18.final, ...), custom_call_target="tpu_custom_call" | custom-call | tf_op jit(solution)/shard_map/write_out/pallas_call | solution.py:377

commit v6 on v5

--- a/solution.py
+++ b/solution.py
@@ -75,7 +75,7 @@
     def load_block(dz):
         at = pl.ds(pl.multiple_of(plane(dz) * LANES, LANES), LANES)
         return pltpu.make_async_copy(
-            gate.at[pl.ds(0, EACH * LANES), at], held.at[0, :, at], block_sem.at[TURNS.index(dz)]
+            gate.at[pl.ds(0, EACH * LANES), at], held.at[0, :, at], block_sem.at[min(abs(dz) + 1, 3) % 3]
         )
 
     for dz in NEAR:
@@ -138,8 +138,12 @@
             news.at[(1 - upward) * 4 + abs(dz)], inc=1, device_id={"zero": target}, device_id_type=MESH
         )
 
+    def blocks_in(count, which):
+        blocks = held.at[0, :, pl.ds(0, count * LANES)]
+        pltpu.make_async_copy(blocks, blocks, block_sem.at[which]).wait()
+
+    blocks_in(2, 2)
     for dz in NEAR[:2]:
-        load_block(dz).wait()
         prepare(0, dz)
     to_pair = pltpu.make_async_remote_copy(
         src_ref=mine, dst_ref=other, send_sem=pair_sem.at[0], recv_sem=pair_sem.at[1],
@@ -179,7 +183,8 @@
         if abs(dz) < 4:
             pass_on(dz)
         if abs(dz) > 1 and dz != -4:
-            load_block(dz).wait()
+            if dz == 2:
+                blocks_in(5, 0)
             for c in range(EARLY):
                 prepare(c, dz)
         for c in range(EARLY if dz != -4 else 0):
@@ -264,10 +269,11 @@
         for other_z in range(1, 8):
             pl.semaphore_signal(everyone, inc=1, device_id={"zero": other_z * 4 + low}, device_id_type=MESH)
 
+    prepare_and_start(4)
     column_wait(1)
     for i in range(3):
         beside_copy(i).start()
-    kept = step(4, kept)
+    kept = take(4 - EARLY, kept)
     prepare_and_start(CHUNKS - 1)
     pltpu.make_async_copy(beside, beside, beside_sem.at[1]).wait()
     for i in range(4):
@@ -363,7 +369,7 @@
             pltpu.SemaphoreType.DMA((2,)),
             pltpu.SemaphoreType.DMA((2,)),
             pltpu.SemaphoreType.REGULAR((8,)),
-            pltpu.SemaphoreType.DMA((8,)),
+            pltpu.SemaphoreType.DMA((3,)),
             pltpu.SemaphoreType.REGULAR,
             pltpu.SemaphoreType.REGULAR,
         ],

time: 81.3 us -> 81.3 us (level)
  no operation moved by 1% of the time
where the time goes in v6:
time: 81.3 us; the launch traced here: 81.2 us
  Pallas kernels  80.5 us (99%)
    pallas_call x1, Pallas kernels, local(): pl.pallas_call(exchange, out_shape=held, in_specs=[pl.BlockSpec(memory_sp...  78.7 us
    pallas_call x1, Pallas kernels, local(): pl.pallas_call(write_out, out_shape=(piece, piece, piece, scale, scale, s...  1.83 us

profile of v6, /device:TPU:1, one launch (start us, length us, event | category | flops | bytes accessed | tf_op | source)
XLA Modules:
  0.0 81.2 jit_solution(932825689100113486)
XLA Ops:
  0.6 78.7 %exchange.1 = (bf16[20,32,2048]{2,1,0:T(8,128)(2,1)S(1)}, bf16[32,2,32,128]{3,2,1,0:T(8,128)(2,1)S(1)}, f32[32,128]{1,0:T(8,128)S(1)}, bf16[8,8,2048]{2,1,0:T(8,128)(2,1)S(1)}) custom-call(f32[512,1024]{1,0:T(8,128)} %bitcast.12, f32[512,1024]{1,0:T(8,128)} %bitcast.13, f32[512,1024]{1,0:T(8,128)} %bitcast.14, f32[8,64]{1,0:T(8,128)} %bitcast.15, ...), custom_call_target="tpu_custom_call" | custom-call | tf_op jit(solution)/shard_map/exchange/pallas_call | solution.py:347
  79.4 1.8 %write_out.1 = (bf16[8,32,2048]{2,1,0:T(8,128)(2,1)}, bf16[8,32,2048]{2,1,0:T(8,128)(2,1)}, bf16[8,32,2048]{2,1,0:T(8,128)(2,1)}, f32[8,32]{1,0:T(8,128)}, f32[8...) custom-call(bf16[20,32,2048]{2,1,0:T(8,128)(2,1)S(1)} %get-tuple-element.18.final, ...), custom_call_target="tpu_custom_call" | custom-call | tf_op jit(solution)/shard_map/write_out/pallas_call | solution.py:383
